TPU v7x, 128 devices: a whole 4x4x4 slice. The times are simulated.
128 devices in a mesh: head: 16 (over z, y), batch: 8 (over x, core).
Axes of the slice: x: 4, y: 4, z: 4, core: 2. Of those that a mesh axis runs over, the one named last changes fastest.
Arguments:
- incoming_hidden_stream: bfloat16 [1024, 4096], P('batch'), may hold values from -6 to 6
- reception_projection: bfloat16 [4096, 4096], P(None, 'head'), may hold values from -0.09375 to 0.09375
- address_projection: bfloat16 [4096, 4096], P(None, 'head'), may hold values from -0.09375 to 0.09375
- payload_projection: bfloat16 [4096, 4096], P(None, 'head'), may hold values from -0.09375 to 0.09375
- sigmoid_filter_matrix: bfloat16 [4096, 4096], P(None, 'head'), may hold values from -0.09375 to 0.09375
- forgetting_speed: float32 [1024, 4096], P('batch', 'head'), may hold values from 0.01 to 1.5
- adaptation_step_size: float32 [1024, 4096], P('batch', 'head'), may hold values from 0 to 1
- diagonal_boost: float32 [4096], P('head'), may hold values from -0.6 to 0.6
- subspace_standardize_scale: float32 [4096], P('head'), may hold values from 0.5 to 2
- recurrent_memory_matrix: float32 [128, 64, 64, 64], P('batch', 'head'), may hold values from -6 to 6
- emission_projection: bfloat16 [4096, 4096], P('head'), may hold values from -0.09375 to 0.09375
- closing_standardize_scale: float32 [4096], replicated, may hold values from 0.7 to 2
- lexicon_projection: bfloat16 [4096, 65536], P(None, ('head', 'batch')), may hold values from -32 to 32
- proposed_tokens_list: int32 [128, 8], P('batch'), may hold values from 0 to 65535
- threshold_milli_nats: int32 [128, 8], P('batch'), may hold values from -22000 to -10001
Outputs:
- new_state: float32 [128, 64, 64, 64], P('batch', 'head')
- margin: float32 [128, 8], P('batch')
- accept: float32 [128, 8], P('batch')
All inputs are finite; a program needn't handle non-finite values.
Results may differ from a plain program's by a relative error of at most 0.0017.
Values may be sent and summed in bfloat16 or wider, within the bound.
A program may use at most 128 MiB of HBM per device.

v0:
```python
import math
import jax
import jax.numpy as jnp
from jax import lax
from jax.sharding import Mesh
from jax.sharding import PartitionSpec as P

HEAD = ("head_0", "head_1")
HEAD_BATCH = ("head_0", "head_1", "batch")


def in_blocks(x, dim, size):
    before, after = (x.shape[:dim], x.shape[dim + 1 :])
    return jnp.moveaxis(x.reshape(*before, size, -1, *after), dim, 0)


def sent_and_summed(x, axis, dim):
    size = lax.axis_size(axis)
    parts = lax.all_to_all(in_blocks(x, dim, size), axis, 0, 0, tiled=True)
    return jnp.sum(parts, axis=0)


def by_axis(x, axes):
    for axis in axes:
        x = lax.psum(x, axis)
    return x


def joined_along(parts, dim):
    parts = jnp.moveaxis(parts, 0, dim)
    shape = parts.shape
    return parts.reshape(*shape[:dim], shape[dim] * shape[dim + 1], *shape[dim + 2 :])


def sent_to_all(x, axis):
    copies = jnp.broadcast_to(x, (lax.axis_size(axis), *x.shape))
    return lax.all_to_all(copies, axis, split_axis=0, concat_axis=0, tiled=True)


def gathered_copies(x, axis, dim):
    return joined_along(sent_to_all(x, axis), dim)


def gathered_once(x, axis):
    leaves = jax.tree.leaves(x)
    sequence = sorted(range(len(leaves)), key=lambda k: -leaves[k].size)
    width = (1, *leaves[sequence[0]].shape)[-1]
    lines = [
        jnp.pad(leaves[k].reshape(-1), (0, -leaves[k].size % width)).reshape(-1, width)
        for k in sequence
    ]
    both, at, found = (sent_to_all(jnp.concatenate(lines), axis), 0, {})
    for k, line in zip(sequence, lines):
        share = both[:, at : at + len(line)].reshape(len(both), -1)
        found[k] = share[:, : leaves[k].size].reshape(-1, *leaves[k].shape)
        at += len(line)
    numbers = iter(range(len(leaves)))
    return jax.tree.map(lambda _: found[next(numbers)], x)


def combined_pairwise(pieces, combine):
    while len(jax.tree.leaves(pieces)[0]) > 1:
        pieces = jax.vmap(combine)(
            *(jax.tree.map(lambda part: part[side::2], pieces) for side in (0, 1))
        )
    return jax.tree.map(lambda part: part[0], pieces)


def combined_all(x, axis, combine):
    pieces = gathered_once(x, axis)
    return combined_pairwise(pieces, combine)


def gathered_by_type(x, axis):
    leaves, found = (jax.tree.leaves(x), {})
    for initial, a in enumerate(leaves):
        if initial not in found:
            alike = [k for k, b in enumerate(leaves) if b.dtype == a.dtype]
            got = (
                gathered_once([leaves[k] for k in alike], axis)
                if len(alike) > 1
                else [sent_to_all(a, axis)]
            )
            for k, b in zip(alike, got):
                found[k] = b
    numbers = iter(range(len(leaves)))
    return jax.tree.map(lambda _: found[next(numbers)], x)


def merged(x, axis, combine):
    pieces = gathered_by_type(x, axis)
    return combined_pairwise(pieces, combine)


def advance(start, reception_vectors, address_vectors, payload_vectors, decay, rate):
    unit = (
        address_vectors
        * lax.rsqrt(jnp.mean(address_vectors * address_vectors, -1, keepdims=True) + 1e-06)
        / math.sqrt(address_vectors.shape[-1])
    )
    inputs = tuple(
        (
            jnp.moveaxis(item, 1, 0)
            for item in (reception_vectors, address_vectors, payload_vectors, decay, unit, rate)
        )
    )

    def step(current, pieces):
        recept_now, keys_now, values_now, decay_now, unit_now, rate_now = pieces
        recall = jnp.einsum("bhij,bhj->bhi", current, unit_now, precision=lax.Precision.HIGHEST)
        current = (
            current * decay_now[:, :, None, :]
            - recall[:, :, :, None] * (unit_now * rate_now)[:, :, None, :]
            + values_now[:, :, :, None] * keys_now[:, :, None, :]
        )
        output = jnp.einsum("bhij,bhj->bhi", current, recept_now, precision=lax.Precision.HIGHEST)
        return (current, output)

    final, outputs = lax.scan(step, start, inputs)
    return (final, jnp.moveaxis(outputs, 0, 1))


def combine_stats(first, second):
    top = jnp.maximum(first[0], second[0])
    summed = first[1] * jnp.exp(first[0] - top) + second[1] * jnp.exp(second[0] - top)
    return (top, summed, first[2] + second[2])


def local_stats(logits, ids_flat, offset):
    peak = jnp.max(logits, -1)
    total = jnp.sum(jnp.exp(logits - peak[:, None]), -1)
    column = lax.broadcasted_iota(jnp.int32, logits.shape, 1)
    target = jnp.sum(jnp.where(column == (ids_flat - offset)[:, None], logits, 0.0), -1)
    return (peak, total, target)


def shards(
    incoming_hidden_stream,
    reception_projection,
    address_projection,
    payload_projection,
    sigmoid_filter_matrix,
    forgetting_speed,
    adaptation_step_size,
    diagonal_boost,
    subspace_standardize_scale,
    recurrent_memory_matrix,
    emission_projection,
    closing_standardize_scale,
    lexicon_projection,
    proposed_tokens_list,
    threshold_milli_nats,
):
    seq_dev, draft_len = proposed_tokens_list.shape
    lanes_on_shard, subspace_size = (
        recurrent_memory_matrix.shape[1],
        recurrent_memory_matrix.shape[2],
    )
    tok_dev = seq_dev * draft_len
    width = incoming_hidden_stream.shape[1]
    shape4 = (seq_dev, draft_len, lanes_on_shard, subspace_size)
    reception_vectors = jnp.dot(
        incoming_hidden_stream, reception_projection, preferred_element_type=jnp.float32
    ).reshape(shape4)
    address_vectors = jnp.dot(
        incoming_hidden_stream, address_projection, preferred_element_type=jnp.float32
    ).reshape(shape4)
    payload_vectors = jnp.dot(
        incoming_hidden_stream, payload_projection, preferred_element_type=jnp.float32
    ).reshape(shape4)
    gate = jnp.dot(
        incoming_hidden_stream, sigmoid_filter_matrix, preferred_element_type=jnp.float32
    )
    decay = jnp.exp(-forgetting_speed).reshape(shape4)
    rate = adaptation_step_size.reshape(shape4)
    new_state, wkv = advance(
        recurrent_memory_matrix, reception_vectors, address_vectors, payload_vectors, decay, rate
    )
    center = wkv - jnp.mean(wkv, -1, keepdims=True)
    interpolated_embedding = (
        center
        * lax.rsqrt(jnp.mean(center * center, -1, keepdims=True) + 1e-05)
        * subspace_standardize_scale.reshape(lanes_on_shard, subspace_size)
    )
    interpolated_embedding = (
        interpolated_embedding
        + jnp.sum(
            reception_vectors
            * address_vectors
            * diagonal_boost.reshape(lanes_on_shard, subspace_size),
            -1,
            keepdims=True,
        )
        * payload_vectors
    )
    gated = (
        interpolated_embedding.reshape(tok_dev, lanes_on_shard * subspace_size)
        * jax.nn.sigmoid(gate)
    ).astype(jnp.bfloat16)
    partial_out = jnp.dot(gated, emission_projection, preferred_element_type=jnp.float32)
    share = sent_and_summed(partial_out, HEAD, 1)
    cols = share.shape[1]
    begin = lax.axis_index(HEAD) * cols
    residual = (
        lax.dynamic_slice_in_dim(incoming_hidden_stream, begin, cols, 1).astype(jnp.float32) + share
    )
    moment_one, moment_two = (
        by_axis(jnp.sum(residual, -1), HEAD),
        by_axis(jnp.sum(residual * residual, -1), HEAD),
    )
    mean_row = moment_one / width
    variance = moment_two / width - mean_row * mean_row
    gain_part = lax.dynamic_slice_in_dim(closing_standardize_scale, begin, cols, 0)
    normed_part = (
        (residual - mean_row[:, None]) * lax.rsqrt(variance + 1e-05)[:, None] * gain_part
    ).astype(jnp.bfloat16)
    normed = gathered_copies(normed_part, HEAD, 1)
    every, every_ids = (
        lax.all_gather(normed, "batch", axis=0, tiled=True),
        lax.all_gather(proposed_tokens_list, "batch", axis=0, tiled=True),
    )
    logits = jnp.dot(every, lexicon_projection, preferred_element_type=jnp.float32)
    vcols = lexicon_projection.shape[1]
    offset = (lax.axis_index(HEAD) * lax.axis_size("batch") + lax.axis_index("batch")) * vcols
    peak, total, target = local_stats(logits, every_ids.reshape(-1), offset)
    peak, total, target = combined_all((peak, total, target), "batch", combine_stats)
    row_begin = lax.axis_index("batch") * tok_dev
    peak = lax.dynamic_slice_in_dim(peak, row_begin, tok_dev, 0)
    total = lax.dynamic_slice_in_dim(total, row_begin, tok_dev, 0)
    target = lax.dynamic_slice_in_dim(target, row_begin, tok_dev, 0)
    top, summed, target = merged((peak, total, target), HEAD, combine_stats)
    logprob = target - (top + jnp.log(summed))
    margin = logprob.reshape(seq_dev, draft_len) - threshold_milli_nats.astype(jnp.float32) / 1000.0
    accept = jnp.cumprod(jax.nn.sigmoid(margin * 0.5), axis=1)
    return (new_state, margin, accept)


def solution(mesh):
    split = Mesh(mesh.devices.reshape(4, 4, mesh.shape["batch"]), ("head_0", "head_1", "batch"))
    return jax.shard_map(
        shards,
        mesh=split,
        in_specs=(
            P("batch", None),
            P(None, HEAD),
            P(None, HEAD),
            P(None, HEAD),
            P(None, HEAD),
            P("batch", HEAD),
            P("batch", HEAD),
            P(HEAD),
            P(HEAD),
            P("batch", HEAD, None, None),
            P(HEAD, None),
            P(),
            P(None, HEAD_BATCH),
            P("batch", None),
            P("batch", None),
        ),
        out_specs=(P("batch", HEAD, None, None), P("batch", None), P("batch", None)),
        check_vma=False,
    )
```

profile of v0, /device:TPU:0, one launch (start us, length us, event | category | flops | bytes accessed | tf_op | source)
XLA Modules:
  0.0 318.9 jit_solution(11417522193714851282)
XLA Ops:
  7.2 3.3 %copy.146 = f32[16,4,64,64]{3,2,1,0:T(8,128)} copy(f32[16,4,64,64]{3,2,1,0:T(8,128)} %param.26) | data formatting | bytes 2097152
  12.3 2.0 fusion.26
  15.2 2.0 fusion.28
  18.2 2.0 multiply_reduce_fusion
  20.5 1.9 copy_bitcast_fusion.2
  22.3 1.8 reshape.126
  24.1 2.0 fusion.27
  27.0 2.0 copy_bitcast_fusion
  29.0 105.4 %while.12 = (s32[]{:T(128)}, f32[16,4,64,64]{3,2,1,0:T(8,128)}, f32[8,16,4,64]{3,2,1,0:T(4,128)S(1)}, f32[8,16,4,64]{3,2,0,1:T(4,128)}, f32[8,16,4,64]{3,2,1,0:T...) while((s32[]{:T(128)}, f32[16,4,64,64]{3,2,1,0:T(8,128)}, ...), condition=%wide.region_2.3_spmd, body=%wide.region_1.2_spmd.sunk | while | flops 7606274 | bytes 13009081 | solution.py:119
  31.5 4.9 %fusion.54 = f32[16,4,1,64]{3,2,1,0:T(1,128)S(1)} fusion(f32[16,4,64,1]{2,3,1,0:T(1,128)S(1)} %bitcast.118, f32[16,4,64,64]{3,2,1,0:T(8,128)} %get-tuple-element.245), kind=kOutput, calls=%fused_computation.79.clone.1 | convolution fusion | flops 3145728 | bytes 1081344 | tf_op jit(solution)/shard_map/while/body/eval_jaxpr/bhij,bhj->bhi/dot_general | solution.py:110
  37.2 1.5 multiply_add_fusion.8
  38.8 3.3 %fusion.55 = f32[16,4,1,64]{3,2,1,0:T(1,128)S(1)} fusion(f32[16,4,64,64]{3,2,1,0:T(8,128)S(1)} %multiply_add_fusion.8, f32[16,4,64,1]{2,3,1,0:T(1,128)S(1)} %bitcast.117), kind=kOutput, calls=%fused_computation.80.clone.1 | convolution fusion | flops 3145728 | bytes 1081344 | tf_op jit(solution)/shard_map/while/body/eval_jaxpr/bhij,bhj->bhi/dot_general | solution.py:116
  44.7 4.9 %fusion.54 = f32[16,4,1,64]{3,2,1,0:T(1,128)S(1)} fusion(f32[16,4,64,1]{2,3,1,0:T(1,128)S(1)} %bitcast.118, f32[16,4,64,64]{3,2,1,0:T(8,128)} %get-tuple-element.245), kind=kOutput, calls=%fused_computation.79.clone.1 | convolution fusion | flops 3145728 | bytes 1081344 | tf_op jit(solution)/shard_map/while/body/eval_jaxpr/bhij,bhj->bhi/dot_general | solution.py:110
  50.4 1.5 multiply_add_fusion.8
  52.0 3.3 %fusion.55 = f32[16,4,1,64]{3,2,1,0:T(1,128)S(1)} fusion(f32[16,4,64,64]{3,2,1,0:T(8,128)S(1)} %multiply_add_fusion.8, f32[16,4,64,1]{2,3,1,0:T(1,128)S(1)} %bitcast.117), kind=kOutput, calls=%fused_computation.80.clone.1 | convolution fusion | flops 3145728 | bytes 1081344 | tf_op jit(solution)/shard_map/while/body/eval_jaxpr/bhij,bhj->bhi/dot_general | solution.py:116
  57.9 4.9 %fusion.54 = f32[16,4,1,64]{3,2,1,0:T(1,128)S(1)} fusion(f32[16,4,64,1]{2,3,1,0:T(1,128)S(1)} %bitcast.118, f32[16,4,64,64]{3,2,1,0:T(8,128)} %get-tuple-element.245), kind=kOutput, calls=%fused_computation.79.clone.1 | convolution fusion | flops 3145728 | bytes 1081344 | tf_op jit(solution)/shard_map/while/body/eval_jaxpr/bhij,bhj->bhi/dot_general | solution.py:110
  63.6 1.5 multiply_add_fusion.8
  65.1 3.3 %fusion.55 = f32[16,4,1,64]{3,2,1,0:T(1,128)S(1)} fusion(f32[16,4,64,64]{3,2,1,0:T(8,128)S(1)} %multiply_add_fusion.8, f32[16,4,64,1]{2,3,1,0:T(1,128)S(1)} %bitcast.117), kind=kOutput, calls=%fused_computation.80.clone.1 | convolution fusion | flops 3145728 | bytes 1081344 | tf_op jit(solution)/shard_map/while/body/eval_jaxpr/bhij,bhj->bhi/dot_general | solution.py:116
  71.0 4.9 %fusion.54 = f32[16,4,1,64]{3,2,1,0:T(1,128)S(1)} fusion(f32[16,4,64,1]{2,3,1,0:T(1,128)S(1)} %bitcast.118, f32[16,4,64,64]{3,2,1,0:T(8,128)} %get-tuple-element.245), kind=kOutput, calls=%fused_computation.79.clone.1 | convolution fusion | flops 3145728 | bytes 1081344 | tf_op jit(solution)/shard_map/while/body/eval_jaxpr/bhij,bhj->bhi/dot_general | solution.py:110
  76.8 1.5 multiply_add_fusion.8
  78.3 3.3 %fusion.55 = f32[16,4,1,64]{3,2,1,0:T(1,128)S(1)} fusion(f32[16,4,64,64]{3,2,1,0:T(8,128)S(1)} %multiply_add_fusion.8, f32[16,4,64,1]{2,3,1,0:T(1,128)S(1)} %bitcast.117), kind=kOutput, calls=%fused_computation.80.clone.1 | convolution fusion | flops 3145728 | bytes 1081344 | tf_op jit(solution)/shard_map/while/body/eval_jaxpr/bhij,bhj->bhi/dot_general | solution.py:116
  84.2 4.9 %fusion.54 = f32[16,4,1,64]{3,2,1,0:T(1,128)S(1)} fusion(f32[16,4,64,1]{2,3,1,0:T(1,128)S(1)} %bitcast.118, f32[16,4,64,64]{3,2,1,0:T(8,128)} %get-tuple-element.245), kind=kOutput, calls=%fused_computation.79.clone.1 | convolution fusion | flops 3145728 | bytes 1081344 | tf_op jit(solution)/shard_map/while/body/eval_jaxpr/bhij,bhj->bhi/dot_general | solution.py:110
  89.9 1.5 multiply_add_fusion.8
  91.5 3.3 %fusion.55 = f32[16,4,1,64]{3,2,1,0:T(1,128)S(1)} fusion(f32[16,4,64,64]{3,2,1,0:T(8,128)S(1)} %multiply_add_fusion.8, f32[16,4,64,1]{2,3,1,0:T(1,128)S(1)} %bitcast.117), kind=kOutput, calls=%fused_computation.80.clone.1 | convolution fusion | flops 3145728 | bytes 1081344 | tf_op jit(solution)/shard_map/while/body/eval_jaxpr/bhij,bhj->bhi/dot_general | solution.py:116
  97.4 4.9 %fusion.54 = f32[16,4,1,64]{3,2,1,0:T(1,128)S(1)} fusion(f32[16,4,64,1]{2,3,1,0:T(1,128)S(1)} %bitcast.118, f32[16,4,64,64]{3,2,1,0:T(8,128)} %get-tuple-element.245), kind=kOutput, calls=%fused_computation.79.clone.1 | convolution fusion | flops 3145728 | bytes 1081344 | tf_op jit(solution)/shard_map/while/body/eval_jaxpr/bhij,bhj->bhi/dot_general | solution.py:110
  103.1 1.5 multiply_add_fusion.8
  104.7 3.3 %fusion.55 = f32[16,4,1,64]{3,2,1,0:T(1,128)S(1)} fusion(f32[16,4,64,64]{3,2,1,0:T(8,128)S(1)} %multiply_add_fusion.8, f32[16,4,64,1]{2,3,1,0:T(1,128)S(1)} %bitcast.117), kind=kOutput, calls=%fused_computation.80.clone.1 | convolution fusion | flops 3145728 | bytes 1081344 | tf_op jit(solution)/shard_map/while/body/eval_jaxpr/bhij,bhj->bhi/dot_general | solution.py:116
  110.6 4.9 %fusion.54 = f32[16,4,1,64]{3,2,1,0:T(1,128)S(1)} fusion(f32[16,4,64,1]{2,3,1,0:T(1,128)S(1)} %bitcast.118, f32[16,4,64,64]{3,2,1,0:T(8,128)} %get-tuple-element.245), kind=kOutput, calls=%fused_computation.79.clone.1 | convolution fusion | flops 3145728 | bytes 1081344 | tf_op jit(solution)/shard_map/while/body/eval_jaxpr/bhij,bhj->bhi/dot_general | solution.py:110
  116.3 1.5 multiply_add_fusion.8
  117.9 3.3 %fusion.55 = f32[16,4,1,64]{3,2,1,0:T(1,128)S(1)} fusion(f32[16,4,64,64]{3,2,1,0:T(8,128)S(1)} %multiply_add_fusion.8, f32[16,4,64,1]{2,3,1,0:T(1,128)S(1)} %bitcast.117), kind=kOutput, calls=%fused_computation.80.clone.1 | convolution fusion | flops 3145728 | bytes 1081344 | tf_op jit(solution)/shard_map/while/body/eval_jaxpr/bhij,bhj->bhi/dot_general | solution.py:116
  123.8 4.9 %fusion.54 = f32[16,4,1,64]{3,2,1,0:T(1,128)S(1)} fusion(f32[16,4,64,1]{2,3,1,0:T(1,128)S(1)} %bitcast.118, f32[16,4,64,64]{3,2,1,0:T(8,128)} %get-tuple-element.245), kind=kOutput, calls=%fused_computation.79.clone.1 | convolution fusion | flops 3145728 | bytes 1081344 | tf_op jit(solution)/shard_map/while/body/eval_jaxpr/bhij,bhj->bhi/dot_general | solution.py:110
  129.5 1.5 multiply_add_fusion.8
  131.1 3.3 %fusion.55 = f32[16,4,1,64]{3,2,1,0:T(1,128)S(1)} fusion(f32[16,4,64,64]{3,2,1,0:T(8,128)S(1)} %multiply_add_fusion.8, f32[16,4,64,1]{2,3,1,0:T(1,128)S(1)} %bitcast.117), kind=kOutput, calls=%fused_computation.80.clone.1 | convolution fusion | flops 3145728 | bytes 1081344 | tf_op jit(solution)/shard_map/while/body/eval_jaxpr/bhij,bhj->bhi/dot_general | solution.py:116
  139.9 4.2 %fusion.5 = f32[128,4096]{1,0:T(8,128)} fusion(bf16[256,4096]{1,0:T(8,128)(2,1)S(1)} %copy-done, f32[128,256]{1,0:T(8,128)S(1)} %reshape.129, bf16[128,4096]{1,0:T(8,128)(2,1)S(1)} %copy-done.3, bf16[4096,256]{1,0:T(8,128)(2,1)} %param.21), kind=kOutput, calls=%fused_computation.18 | convolution fusion | flops 537034752 | bytes 7471104 | tf_op jit(solution)/shard_map/dot_general | solution.py:200
  144.2 3.2 copy.131
  147.3 8.2 %all-to-all-start = ((f32[16,128,256]{2,1,0:T(8,128)}), f32[16,128,256]{2,1,0:T(8,128)}, u32[]{:S(2)}, u32[]{:S(2)}) async-start(f32[16,128,256]{2,1,0:T(8,128)} %bitcast.113), calls=%async_computation | async-start | bytes 4194304 | tf_op jit(solution)/shard_map/all_to_all | solution.py:19
  156.4 31.0 %all-to-all-done = f32[16,128,256]{2,1,0:T(8,128)} async-done(((f32[16,128,256]{2,1,0:T(8,128)}), f32[16,128,256]{2,1,0:T(8,128)}, u32[]{:S(2)}, u32[]{:S(2)}) %all-to-all-start) | async-done | bytes 2097184 | tf_op jit(solution)/shard_map/all_to_all | solution.py:19
  187.4 1.7 reduce_sum.85
  189.2 9.5 %all-reduce.1 = (f32[128]{0:T(128)S(1)}, f32[128]{0:T(128)S(1)}) all-reduce(f32[128]{0:T(128)S(1)} %get-tuple-element.107, f32[128]{0:T(128)S(1)} %get-tuple-element.106), channel_id=1, replica_groups=mesh['head_0'=4,'head_1'=4,'batch'=8] {'head_0'}, use_global_device_ids=true, to_apply=%region_11.12 | all-reduce | flops 256 | bytes 2048 | tf_op jit(solution)/shard_map/psum | solution.py:25
  198.7 7.7 %all-reduce = (f32[128]{0:T(128)S(1)}, f32[128]{0:T(128)S(1)}) all-reduce(f32[128]{0:T(128)S(1)} %get-tuple-element.130, f32[128]{0:T(128)S(1)} %get-tuple-element.131), channel_id=1, replica_groups=mesh['head_0'=4,'head_1'=4,'batch'=8] {'head_1'}, use_global_device_ids=true, to_apply=%region_12.13 | all-reduce | flops 256 | bytes 2048 | tf_op jit(solution)/shard_map/psum | solution.py:25
  206.9 16.6 %all_to_all.20 = bf16[16,128,256]{1,2,0:T(8,128)(2,1)} all-to-all(bf16[16,128,256]{1,2,0:T(8,128)(2,1)S(1)} %broadcast_in_dim.21), channel_id=1, replica_groups=mesh['head_0'=4,'head_1'=4,'batch'=8] {'head_0','head_1'}, dimensions={0} | all-to-all | bytes 2097152 | tf_op jit(solution)/shard_map/all_to_all | solution.py:37
  223.5 13.3 %all-gather = s32[8,16,8]{1,2,0:T(8,128)S(1)} all-gather(s32[1,16,8]{1,2,0:T(8,128)S(1)} %bitcast.136), channel_id=1, replica_groups=mesh['head_0'=4,'head_1'=4,'batch'=8] {'batch'}, dimensions={0}, use_global_device_ids=true | all-gather | bytes 4608 | tf_op jit(solution)/shard_map/all_gather | solution.py:220
  237.0 37.6 %all-gather.3.cloned.1.call-done = bf16[1024,4096]{0,1:T(8,128)(2,1)} async-done(((bf16[128,4096]{0,1:T(8,128)(2,1)}), bf16[1024,4096]{0,1:T(8,128)(2,1)}) %all-gather.3.cloned.1.call-update) | async-done | bytes 8388624 | tf_op jit(solution)/shard_map/all_gather | solution.py:219
  274.6 8.3 %fusion.23 = (f32[1024]{0:T(1024)S(1)}, f32[1024,512]{0,1:T(8,128)S(1)}) fusion(bf16[1024,4096]{0,1:T(8,128)(2,1)} %all-gather.3.cloned.1.call-done, bf16[4096,512]{1,0:T(8,128)(2,1)} %param.29), kind=kOutput, calls=%fused_computation.78 | convolution fusion | flops 4295490560 | bytes 14684160 | tf_op jit(solution)/shard_map/dot_general | solution.py:222
  284.1 4.0 %all-to-all-start.2 = ((f32[8,3,1024]{2,1,0:T(4,128)}), f32[8,3,1024]{2,1,0:T(4,128)S(1)}, u32[]{:S(2)}, u32[]{:S(2)}) async-start(f32[8,3,1024]{2,1,0:T(4,128)} %broadcast_in_dim.23), calls=%async_computation.2 | async-start | bytes 262144 | tf_op jit(solution)/shard_map/all_to_all | solution.py:37
  288.1 6.1 %all-to-all-done.2 = f32[8,3,1024]{2,1,0:T(4,128)S(1)} async-done(((f32[8,3,1024]{2,1,0:T(4,128)}), f32[8,3,1024]{2,1,0:T(4,128)S(1)}, u32[]{:S(2)}, u32[]{:S(2)}) %all-to-all-start.2) | async-done | bytes 98336 | tf_op jit(solution)/shard_map/all_to_all | solution.py:37
  295.4 6.9 %all-to-all-start.3 = ((f32[16,3,128]{2,1,0:T(4,128)}), f32[16,3,128]{2,1,0:T(4,128)S(1)}, u32[]{:S(2)}, u32[]{:S(2)}) async-start(f32[16,3,128]{2,1,0:T(4,128)} %broadcast_in_dim.25), calls=%async_computation.3 | async-start | bytes 65536 | tf_op jit(solution)/shard_map/all_to_all | solution.py:37
  302.5 7.5 %all-to-all-done.3 = f32[16,3,128]{2,1,0:T(4,128)S(1)} async-done(((f32[16,3,128]{2,1,0:T(4,128)}), f32[16,3,128]{2,1,0:T(4,128)S(1)}, u32[]{:S(2)}, u32[]{:S(2)}) %all-to-all-start.3) | async-done | bytes 24608 | tf_op jit(solution)/shard_map/all_to_all | solution.py:37
  (182 shorter events, 42.6 us)
Async XLA Ops:
  7.2 132.8 %copy-start = (bf16[256,4096]{1,0:T(8,128)(2,1)S(1)}, bf16[256,4096]{1,0:T(8,128)(2,1)}, u32[]{:S(2)}) copy-start(bf16[256,4096]{1,0:T(8,128)(2,1)} %param.27) | copy-start | bytes 6291460
  7.2 5.1 %copy-start.3 = (bf16[128,4096]{1,0:T(8,128)(2,1)S(1)}, bf16[128,4096]{1,0:T(8,128)(2,1)}, u32[]{:S(2)}) copy-start(bf16[128,4096]{1,0:T(8,128)(2,1)} %param.17) | copy-start | bytes 3145732
  14.3 3.7 %copy-start.7 = (f32[256]{0:T(256)S(1)}, f32[256]{0:T(256)}, u32[]{:S(2)}) copy-start(f32[256]{0:T(256)} %param.24) | copy-start | bytes 3076
  29.0 105.5 %copy-start.4 = (f32[16,8,4]{2,1,0:T(8,128)S(1)}, f32[16,8,4]{2,1,0:T(8,128)}, u32[]{:S(2)}) copy-start(f32[16,8,4]{2,1,0:T(8,128)} %get-tuple-element.108) | copy-start | bytes 6148
  29.0 106.1 %copy-start.8 = (f32[256]{0:T(256)S(1)}, f32[256]{0:T(256)}, u32[]{:S(2)}) copy-start(f32[256]{0:T(256)} %param.25) | copy-start | bytes 3076
  29.0 8.2 %copy-start.1 = (f32[16,4,64,64]{3,2,1,0:T(8,128)S(1)}, f32[16,4,64,64]{3,2,1,0:T(8,128)}, u32[]{:S(2)}) copy-start(f32[16,4,64,64]{3,2,1,0:T(8,128)} %get-tuple-element.245) | copy-start | bytes 3145732 | tf_op jit(solution)/shard_map/while
  38.8 3.4 %copy-start.2 = (f32[16,4,64,64]{3,2,1,0:T(8,128)}, f32[16,4,64,64]{3,2,1,0:T(8,128)S(1)}, u32[]{:S(2)}) copy-start(f32[16,4,64,64]{3,2,1,0:T(8,128)S(1)} %multiply_add_fusion.8) | copy-start | bytes 3145732 | tf_op jit(solution)/shard_map/while
  42.2 8.2 %copy-start.1 = (f32[16,4,64,64]{3,2,1,0:T(8,128)S(1)}, f32[16,4,64,64]{3,2,1,0:T(8,128)}, u32[]{:S(2)}) copy-start(f32[16,4,64,64]{3,2,1,0:T(8,128)} %get-tuple-element.245) | copy-start | bytes 3145732 | tf_op jit(solution)/shard_map/while
  51.9 3.4 %copy-start.2 = (f32[16,4,64,64]{3,2,1,0:T(8,128)}, f32[16,4,64,64]{3,2,1,0:T(8,128)S(1)}, u32[]{:S(2)}) copy-start(f32[16,4,64,64]{3,2,1,0:T(8,128)S(1)} %multiply_add_fusion.8) | copy-start | bytes 3145732 | tf_op jit(solution)/shard_map/while
  55.3 8.2 %copy-start.1 = (f32[16,4,64,64]{3,2,1,0:T(8,128)S(1)}, f32[16,4,64,64]{3,2,1,0:T(8,128)}, u32[]{:S(2)}) copy-start(f32[16,4,64,64]{3,2,1,0:T(8,128)} %get-tuple-element.245) | copy-start | bytes 3145732 | tf_op jit(solution)/shard_map/while
  65.1 3.4 %copy-start.2 = (f32[16,4,64,64]{3,2,1,0:T(8,128)}, f32[16,4,64,64]{3,2,1,0:T(8,128)S(1)}, u32[]{:S(2)}) copy-start(f32[16,4,64,64]{3,2,1,0:T(8,128)S(1)} %multiply_add_fusion.8) | copy-start | bytes 3145732 | tf_op jit(solution)/shard_map/while
  68.5 8.2 %copy-start.1 = (f32[16,4,64,64]{3,2,1,0:T(8,128)S(1)}, f32[16,4,64,64]{3,2,1,0:T(8,128)}, u32[]{:S(2)}) copy-start(f32[16,4,64,64]{3,2,1,0:T(8,128)} %get-tuple-element.245) | copy-start | bytes 3145732 | tf_op jit(solution)/shard_map/while
  78.3 3.4 %copy-start.2 = (f32[16,4,64,64]{3,2,1,0:T(8,128)}, f32[16,4,64,64]{3,2,1,0:T(8,128)S(1)}, u32[]{:S(2)}) copy-start(f32[16,4,64,64]{3,2,1,0:T(8,128)S(1)} %multiply_add_fusion.8) | copy-start | bytes 3145732 | tf_op jit(solution)/shard_map/while
  81.7 8.2 %copy-start.1 = (f32[16,4,64,64]{3,2,1,0:T(8,128)S(1)}, f32[16,4,64,64]{3,2,1,0:T(8,128)}, u32[]{:S(2)}) copy-start(f32[16,4,64,64]{3,2,1,0:T(8,128)} %get-tuple-element.245) | copy-start | bytes 3145732 | tf_op jit(solution)/shard_map/while
  91.5 3.4 %copy-start.2 = (f32[16,4,64,64]{3,2,1,0:T(8,128)}, f32[16,4,64,64]{3,2,1,0:T(8,128)S(1)}, u32[]{:S(2)}) copy-start(f32[16,4,64,64]{3,2,1,0:T(8,128)S(1)} %multiply_add_fusion.8) | copy-start | bytes 3145732 | tf_op jit(solution)/shard_map/while
  94.9 8.2 %copy-start.1 = (f32[16,4,64,64]{3,2,1,0:T(8,128)S(1)}, f32[16,4,64,64]{3,2,1,0:T(8,128)}, u32[]{:S(2)}) copy-start(f32[16,4,64,64]{3,2,1,0:T(8,128)} %get-tuple-element.245) | copy-start | bytes 3145732 | tf_op jit(solution)/shard_map/while
  104.7 3.4 %copy-start.2 = (f32[16,4,64,64]{3,2,1,0:T(8,128)}, f32[16,4,64,64]{3,2,1,0:T(8,128)S(1)}, u32[]{:S(2)}) copy-start(f32[16,4,64,64]{3,2,1,0:T(8,128)S(1)} %multiply_add_fusion.8) | copy-start | bytes 3145732 | tf_op jit(solution)/shard_map/while
  108.1 8.2 %copy-start.1 = (f32[16,4,64,64]{3,2,1,0:T(8,128)S(1)}, f32[16,4,64,64]{3,2,1,0:T(8,128)}, u32[]{:S(2)}) copy-start(f32[16,4,64,64]{3,2,1,0:T(8,128)} %get-tuple-element.245) | copy-start | bytes 3145732 | tf_op jit(solution)/shard_map/while
  117.9 3.4 %copy-start.2 = (f32[16,4,64,64]{3,2,1,0:T(8,128)}, f32[16,4,64,64]{3,2,1,0:T(8,128)S(1)}, u32[]{:S(2)}) copy-start(f32[16,4,64,64]{3,2,1,0:T(8,128)S(1)} %multiply_add_fusion.8) | copy-start | bytes 3145732 | tf_op jit(solution)/shard_map/while
  121.3 8.2 %copy-start.1 = (f32[16,4,64,64]{3,2,1,0:T(8,128)S(1)}, f32[16,4,64,64]{3,2,1,0:T(8,128)}, u32[]{:S(2)}) copy-start(f32[16,4,64,64]{3,2,1,0:T(8,128)} %get-tuple-element.245) | copy-start | bytes 3145732 | tf_op jit(solution)/shard_map/while
  131.0 3.4 %copy-start.2 = (f32[16,4,64,64]{3,2,1,0:T(8,128)}, f32[16,4,64,64]{3,2,1,0:T(8,128)S(1)}, u32[]{:S(2)}) copy-start(f32[16,4,64,64]{3,2,1,0:T(8,128)S(1)} %multiply_add_fusion.8) | copy-start | bytes 3145732 | tf_op jit(solution)/shard_map/while
  147.3 40.1 %all-to-all-start = ((f32[16,128,256]{2,1,0:T(8,128)}), f32[16,128,256]{2,1,0:T(8,128)}, u32[]{:S(2)}, u32[]{:S(2)}) async-start(f32[16,128,256]{2,1,0:T(8,128)} %bitcast.113), calls=%async_computation | async-start | bytes 4194304 | tf_op jit(solution)/shard_map/all_to_all | solution.py:19
  155.5 119.1 %all-gather.3.cloned.1.call-start = ((), (), s32[]{:S(2)}) async-start(), calls=%async_computation.4 | async-start | bytes 9437184 | tf_op jit(solution)/shard_map/all_gather | solution.py:219
  206.7 16.9 %copy-start.5 = (s32[16,8]{0,1:T(8,128)S(1)}, s32[16,8]{0,1:T(8,128)}, u32[]{:S(2)}) copy-start(s32[16,8]{0,1:T(8,128)} %param.30) | copy-start | bytes 1540
  282.9 19.5 %copy-start.6 = (s32[16,8]{0,1:T(8,128)S(1)}, s32[16,8]{0,1:T(8,128)}, u32[]{:S(2)}) copy-start(s32[16,8]{0,1:T(8,128)} %param.31) | copy-start | bytes 1540
  284.1 10.1 %all-to-all-start.2 = ((f32[8,3,1024]{2,1,0:T(4,128)}), f32[8,3,1024]{2,1,0:T(4,128)S(1)}, u32[]{:S(2)}, u32[]{:S(2)}) async-start(f32[8,3,1024]{2,1,0:T(4,128)} %broadcast_in_dim.23), calls=%async_computation.2 | async-start | bytes 262144 | tf_op jit(solution)/shard_map/all_to_all | solution.py:37
  295.4 14.6 %all-to-all-start.3 = ((f32[16,3,128]{2,1,0:T(4,128)}), f32[16,3,128]{2,1,0:T(4,128)S(1)}, u32[]{:S(2)}, u32[]{:S(2)}) async-start(f32[16,3,128]{2,1,0:T(4,128)} %broadcast_in_dim.25), calls=%async_computation.3 | async-start | bytes 65536 | tf_op jit(solution)/shard_map/all_to_all | solution.py:37
Sparse Core Ops, SparseCore 0:
  223.6 50.9 all-gather.2
where the time goes:
time: 321 us; the launch traced here: 319 us
  matrix products  84.9 us (26%)
  waiting for transfers between devices  82.3 us (26%)
  blocking collectives  47.1 us (15%)
  local copies, waits for them, and re-layouts  41.7 us (13%)
  other arithmetic  29.1 us (9%)
  starting transfers between devices  19.2 us (6%)
  between operations  14.4 us (4%)
    dot_general x8, matrix products, step(): jnp.einsum('bhij,bhj->bhi', current, unit_now, precision=lax.Precision.HI...  39.5 us
    all_gather x1, waiting for transfers between devices, shards(): lax.all_gather(normed, 'batch', axis=0, tiled=True)  37.6 us
    all_to_all x1, waiting for transfers between devices, sent_and_summed(): parts = lax.all_to_all(in_blocks(x, dim, size), axis, 0, 0, tiled=True)  31 us
    dot_general x8, matrix products, step(): jnp.einsum('bhij,bhj->bhi', current, recept_now, precision=lax.Precision....  26.8 us
    psum x2, blocking collectives, by_axis(): x = lax.psum(x, axis)  17.2 us
    all_to_all x1, blocking collectives, sent_to_all(): return lax.all_to_all(copies, axis, split_axis=0, concat_axis=0, tiled=True)  16.6 us
    all_to_all x2, waiting for transfers between devices, sent_to_all(): return lax.all_to_all(copies, axis, split_axis=0, concat_axis=0, tiled=True)  13.6 us
    all_gather x1, blocking collectives, shards(): lax.all_gather(proposed_tokens_list, 'batch', axis=0, tiled=True)  13.3 us
  transfers between devices with their start and end apart: 4, of which 4 were waited for; matrix products, arithmetic and copies ran while one was open for 0% of the time, Pallas kernels for 0%

commit v1 on v0

--- a/solution.py
+++ b/solution.py
@@ -22,7 +22,7 @@
 
 def by_axis(x, axes):
     for axis in axes:
-        x = lax.psum(x, axis)
+        x = jnp.sum(lax.all_gather(x, axis), axis=0)
     return x
 
 

time: 321 us -> 336 us (1.047)
  blocking collectives: 47.1 us -> 62 us
    all_gather x0 -> x4, blocking collectives: none -> 31.9 us  [by_axis(): x = jnp.sum(lax.all_gather(x, axis), axis=0)]
    psum x2 -> x0, blocking collectives: 17.2 us -> none  [by_axis(): x = lax.psum(x, axis)]
where the time goes in v1:
time: 336 us; the launch traced here: 334 us
  matrix products  84.9 us (25%)
  waiting for transfers between devices  82.2 us (24%)
  blocking collectives  62 us (18%)
  local copies, waits for them, and re-layouts  41.6 us (12%)
  other arithmetic  29.1 us (9%)
  starting transfers between devices  19.2 us (6%)
  between operations  14.4 us (4%)
    dot_general x8, matrix products, step(): jnp.einsum('bhij,bhj->bhi', current, unit_now, precision=lax.Precision.HI...  39.5 us
    all_gather x1, waiting for transfers between devices, shards(): lax.all_gather(normed, 'batch', axis=0, tiled=True)  37.5 us
    all_gather x4, blocking collectives, by_axis(): x = jnp.sum(lax.all_gather(x, axis), axis=0)  31.9 us
    all_to_all x1, waiting for transfers between devices, sent_and_summed(): parts = lax.all_to_all(in_blocks(x, dim, size), axis, 0, 0, tiled=True)  31 us
    dot_general x8, matrix products, step(): jnp.einsum('bhij,bhj->bhi', current, recept_now, precision=lax.Precision....  26.8 us
    all_to_all x1, blocking collectives, sent_to_all(): return lax.all_to_all(copies, axis, split_axis=0, concat_axis=0, tiled=True)  16.8 us
    all_to_all x2, waiting for transfers between devices, sent_to_all(): return lax.all_to_all(copies, axis, split_axis=0, concat_axis=0, tiled=True)  13.6 us
    all_gather x1, blocking collectives, shards(): lax.all_gather(proposed_tokens_list, 'batch', axis=0, tiled=True)  13.3 us
  transfers between devices with their start and end apart: 4, of which 4 were waited for; matrix products, arithmetic and copies ran while one was open for 0% of the time, Pallas kernels for 0%

profile of v1, /device:TPU:0, one launch (start us, length us, event | category | flops | bytes accessed | tf_op | source)
XLA Modules:
  0.0 333.9 jit_solution(6656109188221150944)
XLA Ops:
  7.2 3.3 copy.146
  12.3 2.0 fusion.26
  15.2 2.0 fusion.28
  18.2 2.0 multiply_reduce_fusion
  20.4 1.9 copy_bitcast_fusion.2
  22.3 1.8 reshape.136
  24.1 2.0 fusion.27
  27.0 2.0 copy_bitcast_fusion
  29.0 105.4 %while.12 = (s32[]{:T(128)}, f32[16,4,64,64]{3,2,1,0:T(8,128)}, f32[8,16,4,64]{3,2,1,0:T(4,128)S(1)}, f32[8,16,4,64]{3,2,0,1:T(4,128)}, f32[8,16,4,64]{3,2,1,0:T...) while((s32[]{:T(128)}, f32[16,4,64,64]{3,2,1,0:T(8,128)}, ...), condition=%wide.region_2.3_spmd, body=%wide.region_1.2_spmd.sunk | while | flops 7606274 | bytes 13009081 | solution.py:119
  31.5 4.9 %fusion.54 = f32[16,4,1,64]{3,2,1,0:T(1,128)S(1)} fusion(f32[16,4,64,1]{2,3,1,0:T(1,128)S(1)} %bitcast.122, f32[16,4,64,64]{3,2,1,0:T(8,128)} %get-tuple-element.241), kind=kOutput, calls=%fused_computation.79.clone.1 | convolution fusion | flops 3145728 | bytes 1081344 | tf_op jit(solution)/shard_map/while/body/eval_jaxpr/bhij,bhj->bhi/dot_general | solution.py:110
  37.2 1.5 multiply_add_fusion.8
  38.8 3.3 %fusion.55 = f32[16,4,1,64]{3,2,1,0:T(1,128)S(1)} fusion(f32[16,4,64,64]{3,2,1,0:T(8,128)S(1)} %multiply_add_fusion.8, f32[16,4,64,1]{2,3,1,0:T(1,128)S(1)} %bitcast.121), kind=kOutput, calls=%fused_computation.80.clone.1 | convolution fusion | flops 3145728 | bytes 1081344 | tf_op jit(solution)/shard_map/while/body/eval_jaxpr/bhij,bhj->bhi/dot_general | solution.py:116
  44.7 4.9 %fusion.54 = f32[16,4,1,64]{3,2,1,0:T(1,128)S(1)} fusion(f32[16,4,64,1]{2,3,1,0:T(1,128)S(1)} %bitcast.122, f32[16,4,64,64]{3,2,1,0:T(8,128)} %get-tuple-element.241), kind=kOutput, calls=%fused_computation.79.clone.1 | convolution fusion | flops 3145728 | bytes 1081344 | tf_op jit(solution)/shard_map/while/body/eval_jaxpr/bhij,bhj->bhi/dot_general | solution.py:110
  50.4 1.5 multiply_add_fusion.8
  51.9 3.3 %fusion.55 = f32[16,4,1,64]{3,2,1,0:T(1,128)S(1)} fusion(f32[16,4,64,64]{3,2,1,0:T(8,128)S(1)} %multiply_add_fusion.8, f32[16,4,64,1]{2,3,1,0:T(1,128)S(1)} %bitcast.121), kind=kOutput, calls=%fused_computation.80.clone.1 | convolution fusion | flops 3145728 | bytes 1081344 | tf_op jit(solution)/shard_map/while/body/eval_jaxpr/bhij,bhj->bhi/dot_general | solution.py:116
  57.9 4.9 %fusion.54 = f32[16,4,1,64]{3,2,1,0:T(1,128)S(1)} fusion(f32[16,4,64,1]{2,3,1,0:T(1,128)S(1)} %bitcast.122, f32[16,4,64,64]{3,2,1,0:T(8,128)} %get-tuple-element.241), kind=kOutput, calls=%fused_computation.79.clone.1 | convolution fusion | flops 3145728 | bytes 1081344 | tf_op jit(solution)/shard_map/while/body/eval_jaxpr/bhij,bhj->bhi/dot_general | solution.py:110
  63.6 1.5 multiply_add_fusion.8
  65.1 3.3 %fusion.55 = f32[16,4,1,64]{3,2,1,0:T(1,128)S(1)} fusion(f32[16,4,64,64]{3,2,1,0:T(8,128)S(1)} %multiply_add_fusion.8, f32[16,4,64,1]{2,3,1,0:T(1,128)S(1)} %bitcast.121), kind=kOutput, calls=%fused_computation.80.clone.1 | convolution fusion | flops 3145728 | bytes 1081344 | tf_op jit(solution)/shard_map/while/body/eval_jaxpr/bhij,bhj->bhi/dot_general | solution.py:116
  71.0 4.9 %fusion.54 = f32[16,4,1,64]{3,2,1,0:T(1,128)S(1)} fusion(f32[16,4,64,1]{2,3,1,0:T(1,128)S(1)} %bitcast.122, f32[16,4,64,64]{3,2,1,0:T(8,128)} %get-tuple-element.241), kind=kOutput, calls=%fused_computation.79.clone.1 | convolution fusion | flops 3145728 | bytes 1081344 | tf_op jit(solution)/shard_map/while/body/eval_jaxpr/bhij,bhj->bhi/dot_general | solution.py:110
  76.7 1.5 multiply_add_fusion.8
  78.3 3.3 %fusion.55 = f32[16,4,1,64]{3,2,1,0:T(1,128)S(1)} fusion(f32[16,4,64,64]{3,2,1,0:T(8,128)S(1)} %multiply_add_fusion.8, f32[16,4,64,1]{2,3,1,0:T(1,128)S(1)} %bitcast.121), kind=kOutput, calls=%fused_computation.80.clone.1 | convolution fusion | flops 3145728 | bytes 1081344 | tf_op jit(solution)/shard_map/while/body/eval_jaxpr/bhij,bhj->bhi/dot_general | solution.py:116
  84.2 4.9 %fusion.54 = f32[16,4,1,64]{3,2,1,0:T(1,128)S(1)} fusion(f32[16,4,64,1]{2,3,1,0:T(1,128)S(1)} %bitcast.122, f32[16,4,64,64]{3,2,1,0:T(8,128)} %get-tuple-element.241), kind=kOutput, calls=%fused_computation.79.clone.1 | convolution fusion | flops 3145728 | bytes 1081344 | tf_op jit(solution)/shard_map/while/body/eval_jaxpr/bhij,bhj->bhi/dot_general | solution.py:110
  89.9 1.5 multiply_add_fusion.8
  91.5 3.3 %fusion.55 = f32[16,4,1,64]{3,2,1,0:T(1,128)S(1)} fusion(f32[16,4,64,64]{3,2,1,0:T(8,128)S(1)} %multiply_add_fusion.8, f32[16,4,64,1]{2,3,1,0:T(1,128)S(1)} %bitcast.121), kind=kOutput, calls=%fused_computation.80.clone.1 | convolution fusion | flops 3145728 | bytes 1081344 | tf_op jit(solution)/shard_map/while/body/eval_jaxpr/bhij,bhj->bhi/dot_general | solution.py:116
  97.4 4.9 %fusion.54 = f32[16,4,1,64]{3,2,1,0:T(1,128)S(1)} fusion(f32[16,4,64,1]{2,3,1,0:T(1,128)S(1)} %bitcast.122, f32[16,4,64,64]{3,2,1,0:T(8,128)} %get-tuple-element.241), kind=kOutput, calls=%fused_computation.79.clone.1 | convolution fusion | flops 3145728 | bytes 1081344 | tf_op jit(solution)/shard_map/while/body/eval_jaxpr/bhij,bhj->bhi/dot_general | solution.py:110
  103.1 1.5 multiply_add_fusion.8
  104.7 3.3 %fusion.55 = f32[16,4,1,64]{3,2,1,0:T(1,128)S(1)} fusion(f32[16,4,64,64]{3,2,1,0:T(8,128)S(1)} %multiply_add_fusion.8, f32[16,4,64,1]{2,3,1,0:T(1,128)S(1)} %bitcast.121), kind=kOutput, calls=%fused_computation.80.clone.1 | convolution fusion | flops 3145728 | bytes 1081344 | tf_op jit(solution)/shard_map/while/body/eval_jaxpr/bhij,bhj->bhi/dot_general | solution.py:116
  110.6 4.9 %fusion.54 = f32[16,4,1,64]{3,2,1,0:T(1,128)S(1)} fusion(f32[16,4,64,1]{2,3,1,0:T(1,128)S(1)} %bitcast.122, f32[16,4,64,64]{3,2,1,0:T(8,128)} %get-tuple-element.241), kind=kOutput, calls=%fused_computation.79.clone.1 | convolution fusion | flops 3145728 | bytes 1081344 | tf_op jit(solution)/shard_map/while/body/eval_jaxpr/bhij,bhj->bhi/dot_general | solution.py:110
  117.9 3.3 %fusion.55 = f32[16,4,1,64]{3,2,1,0:T(1,128)S(1)} fusion(f32[16,4,64,64]{3,2,1,0:T(8,128)S(1)} %multiply_add_fusion.8, f32[16,4,64,1]{2,3,1,0:T(1,128)S(1)} %bitcast.121), kind=kOutput, calls=%fused_computation.80.clone.1 | convolution fusion | flops 3145728 | bytes 1081344 | tf_op jit(solution)/shard_map/while/body/eval_jaxpr/bhij,bhj->bhi/dot_general | solution.py:116
  123.8 4.9 %fusion.54 = f32[16,4,1,64]{3,2,1,0:T(1,128)S(1)} fusion(f32[16,4,64,1]{2,3,1,0:T(1,128)S(1)} %bitcast.122, f32[16,4,64,64]{3,2,1,0:T(8,128)} %get-tuple-element.241), kind=kOutput, calls=%fused_computation.79.clone.1 | convolution fusion | flops 3145728 | bytes 1081344 | tf_op jit(solution)/shard_map/while/body/eval_jaxpr/bhij,bhj->bhi/dot_general | solution.py:110
  131.0 3.3 %fusion.55 = f32[16,4,1,64]{3,2,1,0:T(1,128)S(1)} fusion(f32[16,4,64,64]{3,2,1,0:T(8,128)S(1)} %multiply_add_fusion.8, f32[16,4,64,1]{2,3,1,0:T(1,128)S(1)} %bitcast.121), kind=kOutput, calls=%fused_computation.80.clone.1 | convolution fusion | flops 3145728 | bytes 1081344 | tf_op jit(solution)/shard_map/while/body/eval_jaxpr/bhij,bhj->bhi/dot_general | solution.py:116
  139.9 4.2 %fusion.5 = f32[128,4096]{1,0:T(8,128)} fusion(bf16[256,4096]{1,0:T(8,128)(2,1)S(1)} %copy-done, f32[128,256]{1,0:T(8,128)S(1)} %reshape.139, bf16[128,4096]{1,0:T(8,128)(2,1)S(1)} %copy-done.3, bf16[4096,256]{1,0:T(8,128)(2,1)} %param.21), kind=kOutput, calls=%fused_computation.18 | convolution fusion | flops 537034752 | bytes 7471104 | tf_op jit(solution)/shard_map/dot_general | solution.py:200
  144.1 3.2 copy.131
  147.3 8.2 %all-to-all-start = ((f32[16,128,256]{2,1,0:T(8,128)}), f32[16,128,256]{2,1,0:T(8,128)}, u32[]{:S(2)}, u32[]{:S(2)}) async-start(f32[16,128,256]{2,1,0:T(8,128)} %bitcast.117), calls=%async_computation | async-start | bytes 4194304 | tf_op jit(solution)/shard_map/all_to_all | solution.py:19
  156.3 31.0 %all-to-all-done = f32[16,128,256]{2,1,0:T(8,128)} async-done(((f32[16,128,256]{2,1,0:T(8,128)}), f32[16,128,256]{2,1,0:T(8,128)}, u32[]{:S(2)}, u32[]{:S(2)}) %all-to-all-start) | async-done | bytes 2097184 | tf_op jit(solution)/shard_map/all_to_all | solution.py:19
  187.4 1.7 reduce_sum.121
  189.2 8.7 %all-gather.4 = f32[4,1,128]{2,1,0:T(1,128)S(1)} all-gather(f32[1,1,128]{2,1,0:T(1,128)S(1)} %bitcast.142), channel_id=2, replica_groups=mesh['head_0'=4,'head_1'=4,'batch'=8] {'head_0'}, dimensions={0}, use_global_device_ids=true | all-gather | bytes 2560 | tf_op jit(solution)/shard_map/all_gather | solution.py:25
  197.9 7.0 %all-gather.5 = f32[4,1,128]{2,1,0:T(1,128)S(1)} all-gather(f32[1,1,128]{2,1,0:T(1,128)S(1)} %bitcast.143), channel_id=3, replica_groups=mesh['head_0'=4,'head_1'=4,'batch'=8] {'head_1'}, dimensions={0}, use_global_device_ids=true | all-gather | bytes 2560 | tf_op jit(solution)/shard_map/all_gather | solution.py:25
  204.9 7.3 %all-gather.6 = f32[4,1,128]{2,1,0:T(1,128)S(1)} all-gather(f32[1,1,128]{2,1,0:T(1,128)S(1)} %bitcast.141), channel_id=4, replica_groups=mesh['head_0'=4,'head_1'=4,'batch'=8] {'head_0'}, dimensions={0}, use_global_device_ids=true | all-gather | bytes 2560 | tf_op jit(solution)/shard_map/all_gather | solution.py:25
  212.2 9.0 %all-gather.7 = f32[4,1,128]{2,1,0:T(1,128)S(1)} all-gather(f32[1,1,128]{2,1,0:T(1,128)S(1)} %bitcast.144), channel_id=5, replica_groups=mesh['head_0'=4,'head_1'=4,'batch'=8] {'head_1'}, dimensions={0}, use_global_device_ids=true | all-gather | bytes 2560 | tf_op jit(solution)/shard_map/all_gather | solution.py:25
  221.7 16.8 %all_to_all.20 = bf16[16,128,256]{1,2,0:T(8,128)(2,1)} all-to-all(bf16[16,128,256]{1,2,0:T(8,128)(2,1)S(1)} %broadcast_in_dim.21), channel_id=1, replica_groups=mesh['head_0'=4,'head_1'=4,'batch'=8] {'head_0','head_1'}, dimensions={0} | all-to-all | bytes 2097152 | tf_op jit(solution)/shard_map/all_to_all | solution.py:37
  238.6 13.3 %all-gather.8 = s32[8,16,8]{1,2,0:T(8,128)S(1)} all-gather(s32[1,16,8]{1,2,0:T(8,128)S(1)} %bitcast.140), channel_id=1, replica_groups=mesh['head_0'=4,'head_1'=4,'batch'=8] {'batch'}, dimensions={0}, use_global_device_ids=true | all-gather | bytes 4608 | tf_op jit(solution)/shard_map/all_gather | solution.py:220
  252.0 37.5 %all-gather.11.cloned.1.call-done = bf16[1024,4096]{0,1:T(8,128)(2,1)} async-done(((bf16[128,4096]{0,1:T(8,128)(2,1)}), bf16[1024,4096]{0,1:T(8,128)(2,1)}) %all-gather.11.cloned.1.call-update) | async-done | bytes 8388624 | tf_op jit(solution)/shard_map/all_gather | solution.py:219
  289.5 8.3 %fusion.23 = (f32[1024]{0:T(1024)S(1)}, f32[1024,512]{0,1:T(8,128)S(1)}) fusion(bf16[1024,4096]{0,1:T(8,128)(2,1)} %all-gather.11.cloned.1.call-done, bf16[4096,512]{1,0:T(8,128)(2,1)} %param.29), kind=kOutput, calls=%fused_computation.78 | convolution fusion | flops 4295490560 | bytes 14684160 | tf_op jit(solution)/shard_map/dot_general | solution.py:222
  299.1 4.0 %all-to-all-start.2 = ((f32[8,3,1024]{2,1,0:T(4,128)}), f32[8,3,1024]{2,1,0:T(4,128)S(1)}, u32[]{:S(2)}, u32[]{:S(2)}) async-start(f32[8,3,1024]{2,1,0:T(4,128)} %broadcast_in_dim.23), calls=%async_computation.2 | async-start | bytes 262144 | tf_op jit(solution)/shard_map/all_to_all | solution.py:37
  303.0 6.1 %all-to-all-done.2 = f32[8,3,1024]{2,1,0:T(4,128)S(1)} async-done(((f32[8,3,1024]{2,1,0:T(4,128)}), f32[8,3,1024]{2,1,0:T(4,128)S(1)}, u32[]{:S(2)}, u32[]{:S(2)}) %all-to-all-start.2) | async-done | bytes 98336 | tf_op jit(solution)/shard_map/all_to_all | solution.py:37
  310.4 7.0 %all-to-all-start.3 = ((f32[16,3,128]{2,1,0:T(4,128)}), f32[16,3,128]{2,1,0:T(4,128)S(1)}, u32[]{:S(2)}, u32[]{:S(2)}) async-start(f32[16,3,128]{2,1,0:T(4,128)} %broadcast_in_dim.25), calls=%async_computation.3 | async-start | bytes 65536 | tf_op jit(solution)/shard_map/all_to_all | solution.py:37
  317.4 7.5 %all-to-all-done.3 = f32[16,3,128]{2,1,0:T(4,128)S(1)} async-done(((f32[16,3,128]{2,1,0:T(4,128)}), f32[16,3,128]{2,1,0:T(4,128)S(1)}, u32[]{:S(2)}, u32[]{:S(2)}) %all-to-all-start.3) | async-done | bytes 24608 | tf_op jit(solution)/shard_map/all_to_all | solution.py:37
  (188 shorter events, 45.7 us)
Async XLA Ops:
  7.2 132.7 %copy-start = (bf16[256,4096]{1,0:T(8,128)(2,1)S(1)}, bf16[256,4096]{1,0:T(8,128)(2,1)}, u32[]{:S(2)}) copy-start(bf16[256,4096]{1,0:T(8,128)(2,1)} %param.27) | copy-start | bytes 6291460
  7.2 5.1 %copy-start.3 = (bf16[128,4096]{1,0:T(8,128)(2,1)S(1)}, bf16[128,4096]{1,0:T(8,128)(2,1)}, u32[]{:S(2)}) copy-start(bf16[128,4096]{1,0:T(8,128)(2,1)} %param.17) | copy-start | bytes 3145732
  14.3 3.8 %copy-start.7 = (f32[256]{0:T(256)S(1)}, f32[256]{0:T(256)}, u32[]{:S(2)}) copy-start(f32[256]{0:T(256)} %param.24) | copy-start | bytes 3076
  29.0 105.5 %copy-start.4 = (f32[16,8,4]{2,1,0:T(8,128)S(1)}, f32[16,8,4]{2,1,0:T(8,128)}, u32[]{:S(2)}) copy-start(f32[16,8,4]{2,1,0:T(8,128)} %get-tuple-element.108) | copy-start | bytes 6148
  29.0 106.1 %copy-start.8 = (f32[256]{0:T(256)S(1)}, f32[256]{0:T(256)}, u32[]{:S(2)}) copy-start(f32[256]{0:T(256)} %param.25) | copy-start | bytes 3076
  29.0 8.2 %copy-start.1 = (f32[16,4,64,64]{3,2,1,0:T(8,128)S(1)}, f32[16,4,64,64]{3,2,1,0:T(8,128)}, u32[]{:S(2)}) copy-start(f32[16,4,64,64]{3,2,1,0:T(8,128)} %get-tuple-element.241) | copy-start | bytes 3145732 | tf_op jit(solution)/shard_map/while
  38.7 3.4 %copy-start.2 = (f32[16,4,64,64]{3,2,1,0:T(8,128)}, f32[16,4,64,64]{3,2,1,0:T(8,128)S(1)}, u32[]{:S(2)}) copy-start(f32[16,4,64,64]{3,2,1,0:T(8,128)S(1)} %multiply_add_fusion.8) | copy-start | bytes 3145732 | tf_op jit(solution)/shard_map/while
  42.1 8.2 %copy-start.1 = (f32[16,4,64,64]{3,2,1,0:T(8,128)S(1)}, f32[16,4,64,64]{3,2,1,0:T(8,128)}, u32[]{:S(2)}) copy-start(f32[16,4,64,64]{3,2,1,0:T(8,128)} %get-tuple-element.241) | copy-start | bytes 3145732 | tf_op jit(solution)/shard_map/while
  51.9 3.4 %copy-start.2 = (f32[16,4,64,64]{3,2,1,0:T(8,128)}, f32[16,4,64,64]{3,2,1,0:T(8,128)S(1)}, u32[]{:S(2)}) copy-start(f32[16,4,64,64]{3,2,1,0:T(8,128)S(1)} %multiply_add_fusion.8) | copy-start | bytes 3145732 | tf_op jit(solution)/shard_map/while
  55.3 8.2 %copy-start.1 = (f32[16,4,64,64]{3,2,1,0:T(8,128)S(1)}, f32[16,4,64,64]{3,2,1,0:T(8,128)}, u32[]{:S(2)}) copy-start(f32[16,4,64,64]{3,2,1,0:T(8,128)} %get-tuple-element.241) | copy-start | bytes 3145732 | tf_op jit(solution)/shard_map/while
  65.1 3.4 %copy-start.2 = (f32[16,4,64,64]{3,2,1,0:T(8,128)}, f32[16,4,64,64]{3,2,1,0:T(8,128)S(1)}, u32[]{:S(2)}) copy-start(f32[16,4,64,64]{3,2,1,0:T(8,128)S(1)} %multiply_add_fusion.8) | copy-start | bytes 3145732 | tf_op jit(solution)/shard_map/while
  68.5 8.2 %copy-start.1 = (f32[16,4,64,64]{3,2,1,0:T(8,128)S(1)}, f32[16,4,64,64]{3,2,1,0:T(8,128)}, u32[]{:S(2)}) copy-start(f32[16,4,64,64]{3,2,1,0:T(8,128)} %get-tuple-element.241) | copy-start | bytes 3145732 | tf_op jit(solution)/shard_map/while
  78.3 3.4 %copy-start.2 = (f32[16,4,64,64]{3,2,1,0:T(8,128)}, f32[16,4,64,64]{3,2,1,0:T(8,128)S(1)}, u32[]{:S(2)}) copy-start(f32[16,4,64,64]{3,2,1,0:T(8,128)S(1)} %multiply_add_fusion.8) | copy-start | bytes 3145732 | tf_op jit(solution)/shard_map/while
  81.7 8.2 %copy-start.1 = (f32[16,4,64,64]{3,2,1,0:T(8,128)S(1)}, f32[16,4,64,64]{3,2,1,0:T(8,128)}, u32[]{:S(2)}) copy-start(f32[16,4,64,64]{3,2,1,0:T(8,128)} %get-tuple-element.241) | copy-start | bytes 3145732 | tf_op jit(solution)/shard_map/while
  91.5 3.4 %copy-start.2 = (f32[16,4,64,64]{3,2,1,0:T(8,128)}, f32[16,4,64,64]{3,2,1,0:T(8,128)S(1)}, u32[]{:S(2)}) copy-start(f32[16,4,64,64]{3,2,1,0:T(8,128)S(1)} %multiply_add_fusion.8) | copy-start | bytes 3145732 | tf_op jit(solution)/shard_map/while
  94.9 8.2 %copy-start.1 = (f32[16,4,64,64]{3,2,1,0:T(8,128)S(1)}, f32[16,4,64,64]{3,2,1,0:T(8,128)}, u32[]{:S(2)}) copy-start(f32[16,4,64,64]{3,2,1,0:T(8,128)} %get-tuple-element.241) | copy-start | bytes 3145732 | tf_op jit(solution)/shard_map/while
  104.7 3.4 %copy-start.2 = (f32[16,4,64,64]{3,2,1,0:T(8,128)}, f32[16,4,64,64]{3,2,1,0:T(8,128)S(1)}, u32[]{:S(2)}) copy-start(f32[16,4,64,64]{3,2,1,0:T(8,128)S(1)} %multiply_add_fusion.8) | copy-start | bytes 3145732 | tf_op jit(solution)/shard_map/while
  108.1 8.2 %copy-start.1 = (f32[16,4,64,64]{3,2,1,0:T(8,128)S(1)}, f32[16,4,64,64]{3,2,1,0:T(8,128)}, u32[]{:S(2)}) copy-start(f32[16,4,64,64]{3,2,1,0:T(8,128)} %get-tuple-element.241) | copy-start | bytes 3145732 | tf_op jit(solution)/shard_map/while
  117.8 3.4 %copy-start.2 = (f32[16,4,64,64]{3,2,1,0:T(8,128)}, f32[16,4,64,64]{3,2,1,0:T(8,128)S(1)}, u32[]{:S(2)}) copy-start(f32[16,4,64,64]{3,2,1,0:T(8,128)S(1)} %multiply_add_fusion.8) | copy-start | bytes 3145732 | tf_op jit(solution)/shard_map/while
  121.2 8.2 %copy-start.1 = (f32[16,4,64,64]{3,2,1,0:T(8,128)S(1)}, f32[16,4,64,64]{3,2,1,0:T(8,128)}, u32[]{:S(2)}) copy-start(f32[16,4,64,64]{3,2,1,0:T(8,128)} %get-tuple-element.241) | copy-start | bytes 3145732 | tf_op jit(solution)/shard_map/while
  131.0 3.4 %copy-start.2 = (f32[16,4,64,64]{3,2,1,0:T(8,128)}, f32[16,4,64,64]{3,2,1,0:T(8,128)S(1)}, u32[]{:S(2)}) copy-start(f32[16,4,64,64]{3,2,1,0:T(8,128)S(1)} %multiply_add_fusion.8) | copy-start | bytes 3145732 | tf_op jit(solution)/shard_map/while
  147.3 40.1 %all-to-all-start = ((f32[16,128,256]{2,1,0:T(8,128)}), f32[16,128,256]{2,1,0:T(8,128)}, u32[]{:S(2)}, u32[]{:S(2)}) async-start(f32[16,128,256]{2,1,0:T(8,128)} %bitcast.117), calls=%async_computation | async-start | bytes 4194304 | tf_op jit(solution)/shard_map/all_to_all | solution.py:19
  155.5 134.0 %all-gather.11.cloned.1.call-start = ((), (), s32[]{:S(2)}) async-start(), calls=%async_computation.4 | async-start | bytes 9437184 | tf_op jit(solution)/shard_map/all_gather | solution.py:219
  221.5 17.1 %copy-start.5 = (s32[16,8]{0,1:T(8,128)S(1)}, s32[16,8]{0,1:T(8,128)}, u32[]{:S(2)}) copy-start(s32[16,8]{0,1:T(8,128)} %param.30) | copy-start | bytes 1540
  297.8 19.5 %copy-start.6 = (s32[16,8]{0,1:T(8,128)S(1)}, s32[16,8]{0,1:T(8,128)}, u32[]{:S(2)}) copy-start(s32[16,8]{0,1:T(8,128)} %param.31) | copy-start | bytes 1540
  299.1 10.1 %all-to-all-start.2 = ((f32[8,3,1024]{2,1,0:T(4,128)}), f32[8,3,1024]{2,1,0:T(4,128)S(1)}, u32[]{:S(2)}, u32[]{:S(2)}) async-start(f32[8,3,1024]{2,1,0:T(4,128)} %broadcast_in_dim.23), calls=%async_computation.2 | async-start | bytes 262144 | tf_op jit(solution)/shard_map/all_to_all | solution.py:37
  310.4 14.6 %all-to-all-start.3 = ((f32[16,3,128]{2,1,0:T(4,128)}), f32[16,3,128]{2,1,0:T(4,128)S(1)}, u32[]{:S(2)}, u32[]{:S(2)}) async-start(f32[16,3,128]{2,1,0:T(4,128)} %broadcast_in_dim.25), calls=%async_computation.3 | async-start | bytes 65536 | tf_op jit(solution)/shard_map/all_to_all | solution.py:37
Sparse Core Ops, SparseCore 0:
  238.7 50.8 all-gather.10
